TPU v7x, 32 devices: a whole 2x2x4 slice. The times are simulated.
32 devices in a mesh: expert: 8 (over y, x, core), hidden: 4 (over z).
Axes of the slice: x: 2, y: 2, z: 4, core: 2. Of those that a mesh axis runs over, the one named last changes fastest.
Arguments:
- weight: bfloat16 [8, 1536, 4096], P('expert', 'hidden'), may hold values from -0.15625 to 0.15625
- scales: float32 [8, 12, 32], P('expert'), may hold values from 0.5 to 2
- act_own: bfloat16 [8, 128, 1536], P('expert', None, 'hidden'), may hold values from -6 to 6
- dy_own: bfloat16 [8, 128, 4096], P('expert'), may hold values from -6 to 6
- own_count: int32 [8], P('expert'), may hold values from 1 to 128, as said below
- act_help: bfloat16 [8, 32, 1536], P('expert', None, 'hidden'), may hold values from -6 to 6
- dy_help: bfloat16 [8, 32, 4096], P('expert'), may hold values from -6 to 6
- help_count: int32 [8], P('expert'), may hold values from 1 to 32, as said below
- hot: int32 [1], replicated, may hold values from 0 to 7
Outputs:
- y_own: bfloat16 [8, 128, 4096], P('expert', None, 'hidden')
- dact_own: bfloat16 [8, 128, 1536], P('expert', None, 'hidden')
- own_grad: bfloat16 [8, 1536, 4096], P('expert', 'hidden')
- y_help: bfloat16 [8, 32, 4096], P('expert', None, 'hidden')
- dact_help: bfloat16 [8, 32, 1536], P('expert', None, 'hidden')
- hot_grad: float32 [1536, 4096], P('hidden', 'expert')
Inputs may be any that keep to these rules, and one draw needn't show every extreme that they name: `own_count`: some expert has exactly 128 live rows. `help_count`: some group has exactly 32 live rows.
All inputs are finite; a program needn't handle non-finite values.
Results may differ from a plain program's by a relative error of at most 0.013.
Values may be sent and summed in bfloat16 or wider, within the bound.
No kernel may reach another device: no remote copies, remote signals or barrier semaphores. Data moves between devices by JAX's collectives and lax.ppermute only.
A program may use at most 64 MiB of HBM per device.

v0:
```python
import jax
import jax.numpy as jnp
from jax import lax
from jax.sharding import PartitionSpec as P

block_edge = 128


def from_root(block, axis, source):
    block = jnp.where(lax.axis_index(axis) == source, block, jnp.zeros_like(block))
    return lax.psum(block, axis)


def dequant(weight, scales, slice_start):
    height = weight.shape[1]
    depth = weight.shape[2]
    blocks = (slice_start + jnp.arange(height, dtype=jnp.int32)) // block_edge
    select = (blocks[:, None] == jnp.arange(scales.shape[1], dtype=jnp.int32)[None, :]).astype(
        jnp.float32
    )
    row_scale = jnp.einsum("fb,ebc->efc", select, scales, precision=lax.Precision.HIGHEST)
    shaped = weight.reshape(weight.shape[0], height, depth // block_edge, block_edge).astype(
        jnp.float32
    )
    shaped = shaped * row_scale[..., None]
    return shaped.reshape(weight.shape).astype(jnp.bfloat16)


def masked(values, count):
    live = jnp.arange(values.shape[1], dtype=jnp.int32)[None, :, None] < count[:, None, None]
    return jnp.where(live, values, jnp.zeros_like(values))


def body(weight, scales, act_own, dy_own, own_count, act_help, dy_help, help_count, hot):
    slice_start = lax.axis_index("hidden") * weight.shape[1]
    own_weight = dequant(weight, scales, slice_start)
    experts_here = weight.shape[0]
    hot_index = hot[0]
    hot_local = hot_index % experts_here
    hot_root = hot_index // experts_here
    own_rows = masked(act_own, own_count)
    own_grads = masked(dy_own, own_count)
    help_rows = masked(act_help, help_count)[0]
    help_grads = masked(dy_help, help_count)[0]
    partial_value = jnp.einsum(
        "erf,efd->erd", own_rows, own_weight, preferred_element_type=jnp.float32
    )
    dact = jnp.einsum("erd,efd->erf", own_grads, own_weight, preferred_element_type=jnp.float32)
    gradient = jnp.einsum("erf,erd->efd", own_rows, own_grads, preferred_element_type=jnp.float32)
    dact_own = dact.astype(jnp.bfloat16)
    own_grad = gradient.astype(jnp.bfloat16)
    chosen = lax.dynamic_index_in_dim(own_weight, hot_local, 0, keepdims=False)
    hot_weight = from_root(chosen, "expert", hot_root)
    help_partial_value = jnp.dot(help_rows, hot_weight, preferred_element_type=jnp.float32)
    dact = lax.dot_general(
        help_grads, hot_weight, (((1,), (1,)), ((), ())), preferred_element_type=jnp.float32
    )
    gradient = lax.dot_general(
        help_rows, help_grads, (((0,), (0,)), ((), ())), preferred_element_type=jnp.float32
    )
    summed = lax.psum_scatter(gradient, "expert", scatter_dimension=1, tiled=True)
    help_partial = help_partial_value[None]
    dact_help = dact.astype(jnp.bfloat16)[None]
    y_own, y_help = (
        lax.psum_scatter(
            partial_value.astype(jnp.bfloat16), "hidden", scatter_dimension=2, tiled=True
        ).astype(jnp.float32),
        lax.psum_scatter(
            help_partial.astype(jnp.bfloat16), "hidden", scatter_dimension=2, tiled=True
        ).astype(jnp.float32),
    )
    return (
        y_own.astype(jnp.bfloat16),
        dact_own,
        own_grad,
        y_help.astype(jnp.bfloat16),
        dact_help,
        summed,
    )


def solution(mesh):
    return jax.shard_map(
        body,
        mesh=mesh,
        in_specs=(
            P("expert", "hidden", None),
            P("expert", None, None),
            P("expert", None, "hidden"),
            P("expert", None, None),
            P("expert"),
            P("expert", None, "hidden"),
            P("expert", None, None),
            P("expert"),
            P(),
        ),
        out_specs=(
            P("expert", None, "hidden"),
            P("expert", None, "hidden"),
            P("expert", "hidden", None),
            P("expert", None, "hidden"),
            P("expert", None, "hidden"),
            P("hidden", "expert"),
        ),
        check_vma=False,
    )
```

profile of v0, /device:TPU:0, one launch (start us, length us, event | category | flops | bytes accessed | tf_op | source)
XLA Modules:
  0.0 194.3 jit_solution(13138229122066029622)
XLA Ops:
  8.0 0.0 all-reduce.2.cloned.1.call-start
  8.1 1.0 fusion.11
  9.1 3.8 %mul.18 = f32[384,32,128]{2,1,0:T(8,128)} broadcast(f32[384,32]{1,0:T(8,128)S(1)} %fusion.11), dimensions={0,1} | broadcast | bytes 6340608 | tf_op jit(solution)/shard_map/mul | solution.py:25
  12.9 7.2 %mul.19 = f32[1,384,4096]{2,1,0:T(8,128)} reshape(f32[384,32,128]{2,1,0:T(8,128)} %mul.18) | data formatting | bytes 12582912 | tf_op jit(solution)/shard_map/mul | solution.py:25
  20.7 6.8 %broadcast_select_fusion = (bf16[384,4096]{1,0:T(8,128)(2,1)}, bf16[384,4096]{1,0:T(8,128)(2,1)S(1)}) fusion(pred[]{:T(512)S(6)} %eq.21, f32[1,384,4096]{2,1,0:T(8,128)} %mul.19, bf16[1,384,4096]{2,1,0:T(8,128)(2,1)} %param.9), kind=kLoop, calls=%fused_computation.8 | loop fusion | flops 6291456 | bytes 15728641 | tf_op jit(solution)/shard_map/jit(_where)/select_n | solution.py:10
  27.5 0.0 all-reduce.2.cloned.1.call-update
  27.6 0.0 reduce-scatter.4.cloned.1.call-start
  28.3 0.1 copy-done.3
  28.4 1.7 fusion.1
  30.1 0.0 reduce-scatter.4.cloned.1.call-update
  30.2 0.0 reduce-scatter.6.cloned.1.call-start
  30.9 68.8 %all-reduce.2.cloned.1.call-done = bf16[384,4096]{1,0:T(8,128)(2,1)} async-done(((bf16[384,4096]{1,0:T(8,128)(2,1)}), bf16[384,4096]{1,0:T(8,128)(2,1)}) %all-reduce.2.cloned.1.call-update) | async-done | bytes 3145744 | tf_op jit(solution)/shard_map/psum | solution.py:11
  99.7 3.3 %fusion.2 = bf16[1,32,4096]{2,1,0:T(8,128)(2,1)} fusion(bf16[384,4096]{1,0:T(8,128)(2,1)} %all-reduce.2.cloned.1.call-done, bf16[1,32,384]{2,1,0:T(8,128)(2,1)S(1)} %copy-done.4, pred[32]{0:T(512)(128)(4,1)S(1)} %iota_compare_fusion.2), kind=kOutput, calls=%fused_computation.6 | convolution fusion | flops 100806656 | bytes 3432480 | tf_op jit(solution)/shard_map/dot_general | solution.py:54
  103.0 0.0 reduce-scatter.6.cloned.1.call-update
  103.1 0.0 reduce-scatter.8.cloned.1.call-start
  103.1 3.7 %fusion.8 = f32[384,4096]{1,0:T(8,128)} fusion(bf16[1,32,4096]{2,1,0:T(8,128)(2,1)S(1)} %copy-done.2, pred[32]{0:T(512)(128)(4,1)S(1)} %iota_compare_fusion.2, bf16[1,32,384]{2,1,0:T(8,128)(2,1)S(1)} %copy-done.4), kind=kOutput, calls=%fused_computation.16 | convolution fusion | flops 100806656 | bytes 6578208 | tf_op jit(solution)/shard_map/dot_general | solution.py:58
  106.8 0.0 reduce-scatter.8.cloned.1.call-update
  106.9 0.0 copy-start.1
  106.9 4.1 %fusion = bf16[1,384,4096]{2,1,0:T(8,128)(2,1)} fusion(bf16[1,128,4096]{2,1,0:T(8,128)(2,1)} %param.12, pred[128]{0:T(512)(128)(4,1)S(1)} %iota_compare_fusion.3, bf16[1,128,384]{2,1,0:T(8,128)(2,1)S(1)} %copy-done.3), kind=kOutput, calls=%fused_computation.2 | convolution fusion | flops 404799488 | bytes 4292736 | tf_op jit(solution)/shard_map/erf,erd->efd/dot_general | solution.py:49
  110.9 1.7 fusion.4
  112.7 0.2 copy-done
  112.8 1.7 fusion.5
  114.5 8.7 %reduce-scatter.6.cloned.1.call-done = bf16[1,32,1024]{2,1,0:T(8,128)(2,1)} async-done(((bf16[1,32,4096]{2,1,0:T(8,128)(2,1)}), bf16[1,32,1024]{2,1,0:T(8,128)(2,1)}) %reduce-scatter.6.cloned.1.call-update) | async-done | bytes 65552 | tf_op jit(solution)/shard_map/reduce_scatter | solution.py:68
  123.2 63.6 %reduce-scatter.8.cloned.1.call-done = f32[384,512]{1,0:T(8,128)} async-done(((f32[384,4096]{1,0:T(8,128)}), f32[384,512]{1,0:T(8,128)}) %reduce-scatter.8.cloned.1.call-update) | async-done | bytes 786448 | tf_op jit(solution)/shard_map/reduce_scatter | solution.py:61
  (11 shorter events, 0.0 us)
Async XLA Ops:
  8.0 91.7 %all-reduce.2.cloned.1.call-start = ((), (), s32[]{:S(2)}) async-start(), calls=%async_computation.4 | async-start | bytes 6291456 | tf_op jit(solution)/shard_map/psum | solution.py:11
  27.5 0.9 copy-start.3
  27.6 72.2 %copy-start.4 = (bf16[1,32,384]{2,1,0:T(8,128)(2,1)S(1)}, bf16[1,32,384]{2,1,0:T(8,128)(2,1)}, u32[]{:S(2)}) copy-start(bf16[1,32,384]{2,1,0:T(8,128)(2,1)} %param.14) | copy-start | bytes 73732
  27.6 86.9 %reduce-scatter.4.cloned.1.call-start = ((), (), s32[]{:S(2)}) async-start(), calls=%async_computation.3 | async-start | bytes 1310720 | tf_op jit(solution)/shard_map/reduce_scatter | solution.py:65
  30.1 73.0 %copy-start.2 = (bf16[1,32,4096]{2,1,0:T(8,128)(2,1)S(1)}, bf16[1,32,4096]{2,1,0:T(8,128)(2,1)}, u32[]{:S(2)}) copy-start(bf16[1,32,4096]{2,1,0:T(8,128)(2,1)} %param.15) | copy-start | bytes 786436
  30.2 93.0 %reduce-scatter.6.cloned.1.call-start = ((), (), s32[]{:S(2)}) async-start(), calls=%async_computation.5 | async-start | bytes 327680 | tf_op jit(solution)/shard_map/reduce_scatter | solution.py:68
  103.1 83.7 %reduce-scatter.8.cloned.1.call-start = ((), (), s32[]{:S(2)}) async-start(), calls=%async_computation.6 | async-start | bytes 7077888 | tf_op jit(solution)/shard_map/reduce_scatter | solution.py:61
  106.9 4.1 %copy-start.1 = (bf16[1,128,4096]{2,1,0:T(8,128)(2,1)S(1)}, bf16[1,128,4096]{2,1,0:T(8,128)(2,1)}, u32[]{:S(2)}) copy-start(bf16[1,128,4096]{2,1,0:T(8,128)(2,1)} %param.12) | copy-start | bytes 3145732
  110.9 1.9 copy-start
Sparse Core Ops, SparseCore 0:
  27.7 72.0 all-reduce.1
Sparse Core Ops, SparseCore 1:
  30.9 29.9 reduce-scatter.3
  103.1 20.0 reduce-scatter.5
  127.0 59.7 reduce-scatter.7
where the time goes:
time: 195 us; the launch traced here: 194 us
  waiting for transfers between devices  141 us (72%)
  between operations  17.7 us (9%)
  matrix products  17.2 us (9%)
  local copies, waits for them, and re-layouts  11.3 us (6%)
  other arithmetic  6.87 us (4%)
    psum x1, waiting for transfers between devices, from_root(): return lax.psum(block, axis)  68.8 us
    reduce_scatter x1, waiting for transfers between devices, body(): lax.psum_scatter(gradient, 'expert', scatter_dimension=1, tiled=True)  63.6 us
    mul x2, local copies, waits for them, and re-layouts, dequant(): shaped = shaped * row_scale[..., None]  11 us
    reduce_scatter x1, waiting for transfers between devices, body(): lax.psum_scatter(help_partial.astype(jnp.bfloat16), 'hidden', scatter_dim...  8.65 us
    select_n x1, other arithmetic, from_root(): jnp.where(lax.axis_index(axis) == source, block, jnp.zeros_like(block))  6.85 us
    dot_general x1, matrix products, body(): jnp.einsum('erf,erd->efd', own_rows, own_grads, preferred_element_type=jn...  4.06 us
  transfers between devices with their start and end apart: 4, of which 3 were waited for; matrix products, arithmetic and copies ran while one was open for 8% of the time, Pallas kernels for 0%

commit v1 on v0

--- a/solution.py
+++ b/solution.py
@@ -6,9 +6,14 @@
 block_edge = 128
 
 
+def _point_classes(q_in, axis_name):
+    k_now = jnp.sum(lax.all_gather(q_in, axis_name), 0)
+    return k_now
+
+
 def from_root(block, axis, source):
     block = jnp.where(lax.axis_index(axis) == source, block, jnp.zeros_like(block))
-    return lax.psum(block, axis)
+    return _point_classes(block, axis)
 
 
 def dequant(weight, scales, slice_start):

time: 195 us -> 219 us (1.12)
  other arithmetic: 6.87 us -> 20.4 us
  waiting for transfers between devices: 141 us -> 152 us
    all_gather x0 -> x1, waiting for transfers between devices: none -> 121 us  [_point_classes(): k_now = jnp.sum(lax.all_gather(q_in, axis_name), 0)]
    psum x1 -> x0, waiting for transfers between devices: 68.8 us -> none  [from_root(): return lax.psum(block, axis)]
    reduce_scatter x1, waiting for transfers between devices: 63.6 us -> 8.9 us  [body(): lax.psum_scatter(gradient, 'expert', scatter_dimension=1, tiled=True)]
    reduce_scatter x1, waiting for transfers between devices: 8.65 us -> 22.6 us  [body(): lax.psum_scatter(help_partial.astype(jnp.bfloat16), 'hidden', scatter_dim...]
    reduce_sum x0 -> x1, other arithmetic: none -> 13.5 us  [_point_classes(): k_now = jnp.sum(lax.all_gather(q_in, axis_name), 0)]
    dot_general x1, matrix products: 1.71 us -> 4.01 us  [body(): jnp.einsum('erd,efd->erf', own_grads, own_weight, preferred_element_type=...]
  transfers between devices with their start and end apart: 4 -> 4, of which waited for: 3 -> 3; matrix products, arithmetic and copies ran while one was open for 8% -> 13% of each run, Pallas kernels for 0% -> 0%
where the time goes in v1:
time: 219 us; the launch traced here: 218 us
  waiting for transfers between devices  152 us (69%)
  other arithmetic  20.4 us (9%)
  between operations  18.1 us (8%)
  matrix products  16.4 us (7%)
  local copies, waits for them, and re-layouts  11 us (5%)
    all_gather x1, waiting for transfers between devices, _point_classes(): k_now = jnp.sum(lax.all_gather(q_in, axis_name), 0)  121 us
    reduce_scatter x1, waiting for transfers between devices, body(): lax.psum_scatter(help_partial.astype(jnp.bfloat16), 'hidden', scatter_dim...  22.6 us
    reduce_sum x1, other arithmetic, _point_classes(): k_now = jnp.sum(lax.all_gather(q_in, axis_name), 0)  13.5 us
    mul x2, local copies, waits for them, and re-layouts, dequant(): shaped = shaped * row_scale[..., None]  11 us
    reduce_scatter x1, waiting for transfers between devices, body(): lax.psum_scatter(gradient, 'expert', scatter_dimension=1, tiled=True)  8.9 us
    select_n x1, other arithmetic, from_root(): jnp.where(lax.axis_index(axis) == source, block, jnp.zeros_like(block))  6.85 us
  transfers between devices with their start and end apart: 4, of which 3 were waited for; matrix products, arithmetic and copies ran while one was open for 13% of the time, Pallas kernels for 0%

profile of v1, /device:TPU:0, one launch (start us, length us, event | category | flops | bytes accessed | tf_op | source)
XLA Modules:
  0.0 218.5 jit_solution(1845318768002982627)
XLA Ops:
  8.0 0.0 all-gather.2.cloned.1.call-start
  8.1 1.0 fusion.18
  9.1 3.8 %mul.18 = f32[384,32,128]{2,1,0:T(8,128)} broadcast(f32[384,32]{1,0:T(8,128)S(1)} %fusion.18), dimensions={0,1} | broadcast | bytes 6340608 | tf_op jit(solution)/shard_map/mul | solution.py:30
  12.9 7.2 %mul.19 = f32[1,384,4096]{2,1,0:T(8,128)} reshape(f32[384,32,128]{2,1,0:T(8,128)} %mul.18) | data formatting | bytes 12582912 | tf_op jit(solution)/shard_map/mul | solution.py:30
  20.7 6.8 %broadcast_select_fusion = (bf16[1,384,4096]{2,1,0:T(8,128)(2,1)}, bf16[1,384,4096]{2,1,0:T(8,128)(2,1)S(1)}) fusion(pred[]{:T(512)S(6)} %eq.21, f32[1,384,4096]{2,1,0:T(8,128)} %mul.19, bf16[1,384,4096]{2,1,0:T(8,128)(2,1)} %param.9), kind=kLoop, calls=%fused_computation.10 | loop fusion | flops 6291456 | bytes 15728641 | tf_op jit(solution)/shard_map/jit(_where)/select_n | solution.py:15
  27.5 0.0 all-gather.2.cloned.1.call-update
  27.6 0.0 copy-start.2
  27.6 0.0 copy-start.4
  27.6 0.0 reduce-scatter.4.cloned.1.call-start
  28.7 1.8 fusion.1
  30.5 0.0 reduce-scatter.4.cloned.1.call-update
  30.5 0.0 reduce-scatter.8.cloned.1.call-start
  31.2 3.8 %fusion.15 = f32[384,4096]{1,0:T(8,128)} fusion(bf16[1,32,4096]{2,1,0:T(8,128)(2,1)S(1)} %copy-done.2, pred[32]{0:T(512)(128)(4,1)S(1)} %iota_compare_fusion.2, bf16[1,32,384]{2,1,0:T(8,128)(2,1)S(1)} %copy-done.4), kind=kOutput, calls=%fused_computation.18 | convolution fusion | flops 100806656 | bytes 6578208 | tf_op jit(solution)/shard_map/dot_general | solution.py:63
  35.0 0.0 reduce-scatter.8.cloned.1.call-update
  35.0 0.0 reduce-scatter.6.cloned.1.call-start
  35.1 120.9 %all-gather.2.cloned.1.call-done = bf16[8,384,4096]{2,1,0:T(8,128)(2,1)} async-done(((bf16[1,384,4096]{2,1,0:T(8,128)(2,1)}), bf16[8,384,4096]{2,1,0:T(8,128)(2,1)}) %all-gather.2.cloned.1.call-update) | async-done | bytes 25165840 | tf_op jit(solution)/shard_map/all_gather | solution.py:10
  156.0 13.5 %reduce_sum.12 = bf16[384,4096]{1,0:T(8,128)(2,1)S(1)} reduce(bf16[8,384,4096]{2,1,0:T(8,128)(2,1)} %all-gather.2.cloned.1.call-done, bf16[]{:T(256)} %constant.47.clone.1), dimensions={0}, to_apply=%region_1.2 | reduce | flops 11010048 | bytes 28311554 | tf_op jit(solution)/shard_map/reduce_sum | solution.py:10
  169.5 1.4 fusion.2
  170.9 0.0 reduce-scatter.6.cloned.1.call-update
  170.9 4.0 %fusion.9 = bf16[1,128,384]{2,1,0:T(8,128)(2,1)} fusion(bf16[1,384,4096]{2,1,0:T(8,128)(2,1)} %copy-done, bf16[1,128,4096]{2,1,0:T(8,128)(2,1)} %param.12, pred[128]{0:T(512)(128)(4,1)S(1)} %iota_compare_fusion.3), kind=kOutput, calls=%fused_computation.12 | convolution fusion | flops 403226624 | bytes 4292736 | tf_op jit(solution)/shard_map/erd,efd->erf/dot_general | solution.py:53
  174.9 2.7 %fusion = bf16[1,384,4096]{2,1,0:T(8,128)(2,1)} fusion(bf16[1,128,4096]{2,1,0:T(8,128)(2,1)S(1)} %copy-done.1, pred[128]{0:T(512)(128)(4,1)S(1)} %iota_compare_fusion.3, bf16[1,128,384]{2,1,0:T(8,128)(2,1)S(1)} %copy-done.3), kind=kOutput, calls=%fused_computation.2 | convolution fusion | flops 404799488 | bytes 4292736 | tf_op jit(solution)/shard_map/erf,erd->efd/dot_general | solution.py:54
  177.7 1.7 fusion.12
  179.3 8.9 %reduce-scatter.8.cloned.1.call-done = f32[384,512]{1,0:T(8,128)} async-done(((f32[384,4096]{1,0:T(8,128)}), f32[384,512]{1,0:T(8,128)}) %reduce-scatter.8.cloned.1.call-update) | async-done | bytes 786448 | tf_op jit(solution)/shard_map/reduce_scatter | solution.py:66
  188.2 22.6 %reduce-scatter.6.cloned.1.call-done = bf16[1,32,1024]{2,1,0:T(8,128)(2,1)} async-done(((bf16[1,32,4096]{2,1,0:T(8,128)(2,1)}), bf16[1,32,1024]{2,1,0:T(8,128)(2,1)}) %reduce-scatter.6.cloned.1.call-update) | async-done | bytes 65552 | tf_op jit(solution)/shard_map/reduce_scatter | solution.py:73
  (12 shorter events, 0.0 us)
Async XLA Ops:
  8.0 148.0 %all-gather.2.cloned.1.call-start = ((), (), s32[]{:S(2)}) async-start(), calls=%async_computation.4 | async-start | bytes 28311552 | tf_op jit(solution)/shard_map/all_gather | solution.py:10
  27.5 3.0 %copy-start = (bf16[1,384,4096]{2,1,0:T(8,128)(2,1)}, bf16[1,384,4096]{2,1,0:T(8,128)(2,1)S(1)}, u32[]{:S(2)}) copy-start(bf16[1,384,4096]{2,1,0:T(8,128)(2,1)S(1)} %get-tuple-element.7) | copy-start | bytes 9437188
  27.5 1.2 copy-start.3
  27.6 3.7 %copy-start.2 = (bf16[1,32,4096]{2,1,0:T(8,128)(2,1)S(1)}, bf16[1,32,4096]{2,1,0:T(8,128)(2,1)}, u32[]{:S(2)}) copy-start(bf16[1,32,4096]{2,1,0:T(8,128)(2,1)} %param.15) | copy-start | bytes 786436
  27.6 3.7 %copy-start.4 = (bf16[1,32,384]{2,1,0:T(8,128)(2,1)S(1)}, bf16[1,32,384]{2,1,0:T(8,128)(2,1)}, u32[]{:S(2)}) copy-start(bf16[1,32,384]{2,1,0:T(8,128)(2,1)} %param.14) | copy-start | bytes 73732
  27.6 151.8 %reduce-scatter.4.cloned.1.call-start = ((), (), s32[]{:S(2)}) async-start(), calls=%async_computation.3 | async-start | bytes 1310720 | tf_op jit(solution)/shard_map/reduce_scatter | solution.py:70
  30.5 157.7 %reduce-scatter.8.cloned.1.call-start = ((), (), s32[]{:S(2)}) async-start(), calls=%async_computation.6 | async-start | bytes 7077888 | tf_op jit(solution)/shard_map/reduce_scatter | solution.py:66
  35.0 175.8 %reduce-scatter.6.cloned.1.call-start = ((), (), s32[]{:S(2)}) async-start(), calls=%async_computation.5 | async-start | bytes 327680 | tf_op jit(solution)/shard_map/reduce_scatter | solution.py:73
  170.9 4.0 %copy-start.1 = (bf16[1,128,4096]{2,1,0:T(8,128)(2,1)S(1)}, bf16[1,128,4096]{2,1,0:T(8,128)(2,1)}, u32[]{:S(2)}) copy-start(bf16[1,128,4096]{2,1,0:T(8,128)(2,1)} %param.12) | copy-start | bytes 3145732
Sparse Core Ops, SparseCore 0:
  27.7 128.2 all-gather.1
Sparse Core Ops, SparseCore 1:
  30.9 29.9 reduce-scatter.3
  64.7 123.4 reduce-scatter.7
  190.9 19.9 reduce-scatter.5
